TPU v7x, 32 devices: a whole 2x2x4 slice. The times are simulated.
32 devices in a mesh: gx: 4 (over z), gy: 8 (over y, x, core).
Axes of the slice: x: 2, y: 2, z: 4, core: 2. Of those that a mesh axis runs over, the one named last changes fastest.
Arguments:
- stored_vectors: bfloat16 [2, 16, 32, 4096], P(None, None, 'gx', 'gy'), may hold values from -4 to 4
- disorder: float32 [2, 32, 4096], P(None, 'gx', 'gy'), may hold values from -1.5 to 1.5
- vacancy: int32 [2, 32, 4096], P(None, 'gx', 'gy'), may hold values 0 or 1
- plan: int32 [32], replicated, may hold values from 0 to 31, as said below
Outputs:
- local_moments: float32 [4, 2, 32, 4096], P(None, None, 'gx', 'gy')
- trace_moments: float32 [4, 16], replicated
Inputs may be any that keep to these rules, and one draw needn't show every extreme that they name: plan is a permutation of 0 to 31; stored block b is held by the device at gy index b // 4. The 4 lattice blocks of one device come from 4 different devices, and the 4 stored blocks of one device go to 4 different devices.
All inputs are finite; a program needn't handle non-finite values. No bound on the sum of `vacancy` on one device may be relied on, other than what follows from the above.
Results may differ from a plain program's by a relative error of at most 0.0003.
Values may be sent and summed in bfloat16 or wider, within the bound.
A program may use at most 64 MiB of HBM per device.

v0:
```python
import functools

import jax
import jax.numpy as jnp
from jax import lax
from jax.experimental import pallas as pl
from jax.experimental.pallas import tpu as pltpu
from jax.sharding import PartitionSpec as P

BLOCK = 128
TERMS = 4
HOP_NEXT = 0.3
TWIST_COS = 0.4535961214255773
TWIST_SIN = 0.8912073600614354
SPREAD = 6.5
HALO = TERMS
MESH = pl.DeviceIdType.MESH
F32 = jnp.float32

WAYS = tuple((a, b) for a in (-1, 0, 1) for b in (-1, 0, 1) if (a, b) != (0, 0))


def rows_from(a, wide):
    if a == 0:
        return slice(HALO, HALO + wide)
    return slice(0, HALO) if a == 1 else slice(HALO + wide, 2 * HALO + wide)


def rows_to(a, wide):
    if a == 0:
        return slice(0, wide)
    return slice(wide - HALO, wide) if a == 1 else slice(0, HALO)


def program(
    nx, ny,
    plan_ref, stored_ref, disorder_ref, vacancy_ref,
    moments_ref, trace_ref,
    turned, send, recv, lattice, side, level_x, level_y, vac_x, vac_y, keep_ref, onsite, factor,
    real0, real1, real2, real3, imag1, imag2, imag3, traces, packs, part, parts_y, parts_x,
    a2a_send, a2a_recv, halo_send, halo_recv, site_send, site_recv, sum_send, sum_recv,
):
    gx, gy = lax.axis_index("gx"), lax.axis_index("gy")
    wide, long = disorder_ref.shape[1], disorder_ref.shape[2]
    tall, vectors = lattice.shape[1:3]
    extent = long + BLOCK
    blocks = long // BLOCK
    halves = vectors // 8
    cos, sin = HOP_NEXT * TWIST_COS, HOP_NEXT * TWIST_SIN

    def at(a, b):
        return (lax.rem(gx + a + nx, nx), lax.rem(gy + b + ny, ny))

    def copy(source, target, out_sem, in_sem, device):
        return pltpu.make_async_remote_copy(
            src_ref=source, dst_ref=target, send_sem=out_sem, recv_sem=in_sem,
            device_id=device, device_id_type=MESH,
        )

    barrier = pltpu.get_barrier_semaphore()
    greeted = [at(0, i) for i in range(1, ny)] + [at(i, 0) for i in range(1, nx)]
    greeted += [at(a, b) for a, b in WAYS if a != 0 and b != 0]
    for device in greeted:
        pl.semaphore_signal(barrier, inc=1, device_id=device, device_id_type=MESH)

    for k in range(blocks):
        for s in range(2):
            piece = stored_ref[s, :, :, k * BLOCK : (k + 1) * BLOCK].astype(F32)
            turned[k, s] = jnp.transpose(piece, (1, 0, 2)).astype(jnp.bfloat16)

    def fill(target, place):
        block = turned[0]
        for k in range(1, blocks):
            wanted = plan_ref[target * blocks] == gy * blocks + k
            for j in range(1, blocks):
                wanted = wanted | (plan_ref[target * blocks + j] == gy * blocks + k)
            block = jnp.where(wanted, turned[k], block)
        place[...] = block

    for i in range(1, ny):
        fill(lax.rem(gy + i, ny), send.at[i])
    pl.semaphore_wait(barrier, len(greeted))
    moves = []
    for i in range(1, ny):
        move = copy(send.at[i], recv.at[gy], a2a_send.at[i], a2a_recv.at[i], at(0, i))
        move.start()
        moves.append(move)
    sites = []
    for w, (a, b) in enumerate(WAYS):
        lanes = slice(0, long) if b == 0 else (
            slice(long - BLOCK, long) if b == 1 else slice(0, BLOCK))
        for t, (own, by_x, by_y) in enumerate(
            ((disorder_ref, level_x, level_y), (vacancy_ref, vac_x, vac_y))
        ):
            target = by_x.at[w] if b == 0 else by_y.at[w]
            move = copy(own.at[:, :, lanes], target, site_send.at[w, t], site_recv.at[w, t],
                        at(a, b))
            move.start()
            sites.append(move)
    fill(gy, recv.at[gy])
    traces[...] = jnp.zeros_like(traces)

    for move in moves:
        move.wait()
    for k in range(blocks):
        stored = plan_ref[gy * blocks + k]
        block = recv[0]
        for p in range(1, ny):
            block = jnp.where(stored >= p * blocks, recv[p], block)
        lattice[:, HALO : HALO + wide, :, k * BLOCK : (k + 1) * BLOCK] = block
    lane = lax.broadcasted_iota(jnp.int32, (vectors, BLOCK), 1)
    first = jnp.zeros((vectors, BLOCK), F32)
    last = jnp.zeros((vectors, BLOCK), F32)
    for s in range(2):
        for x in range(wide):
            shift = HALO * (s * wide + x)
            tile = lattice[s, HALO + x, :, 0:BLOCK].astype(F32)
            first = first + pltpu.roll(jnp.where(lane < HALO, tile, 0.0), shift, axis=1)
            tile = lattice[s, HALO + x, :, long - BLOCK : long].astype(F32)
            last = last + pltpu.roll(jnp.where(lane >= BLOCK - HALO, tile, 0.0), shift, axis=1)
    packs[0] = first.astype(jnp.bfloat16)
    packs[1] = last.astype(jnp.bfloat16)
    halos = {}
    for a, b in ((0, 1), (0, -1), (1, 0), (-1, 0), (1, 1), (1, -1), (-1, 1), (-1, -1)):
        w = WAYS.index((a, b))
        if b == 0:
            own = rows_to(a, wide)
            source = lattice.at[:, own.start + HALO : own.stop + HALO]
            target = lattice.at[:, rows_from(a, wide)]
        else:
            source, target = packs.at[0 if b == -1 else 1], side.at[w]
        halos[a, b] = copy(source, target, halo_send.at[w], halo_recv.at[w], at(a, b))
        halos[a, b].start()

    for move in sites:
        move.wait()
    low = lax.broadcasted_iota(jnp.int32, (2, wide, BLOCK), 2) < BLOCK // 2
    for own, by_x, by_y, out in (
        (disorder_ref, level_x, level_y, onsite),
        (vacancy_ref, vac_x, vac_y, keep_ref),
    ):
        for a in (-1, 0, 1):
            middle = own[...] if a == 0 else by_x[WAYS.index((a, 0))]
            edge = jnp.where(low, by_y[WAYS.index((a, -1))], by_y[WAYS.index((a, 1))])
            kept = rows_to(a, wide)
            out[:, rows_from(a, wide), 0:long] = middle[:, kept].astype(F32)
            out[:, rows_from(a, wide), long:] = edge[:, kept].astype(F32)
    factor[...] = keep_ref[...] * (1.0 / SPREAD)
    onsite[...] = onsite[...] * factor[...]

    def begin(a):
        rows, own = rows_from(a, wide), rows_to(a, wide)
        for s in range(2):
            for x in range(rows.start, rows.stop):
                mask = keep_ref[s, x : x + 1, :]
                shift = HALO * (s * wide + own.start + x - rows.start)
                shift = (BLOCK - shift) % BLOCK
                real0[s, x, :, 0:long] = lattice[s, x].astype(F32) * mask[:, 0:long]
                right = pltpu.roll(side[WAYS.index((a, -1))].astype(F32), shift, axis=1)
                left = pltpu.roll(side[WAYS.index((a, 1))].astype(F32), shift, axis=1)
                edge = jnp.where(lane < BLOCK // 2, right, left)
                real0[s, x, :, long:] = edge * mask[:, long:]

    def back(value):
        return pltpu.roll(value, 1, axis=1)

    def ahead(value):
        return pltpu.roll(value, extent - 1, axis=1)

    def bond(r, i, first, second, chiral, want_imag):
        turn = chiral * sin
        out_real = cos * (r[first] + r[second])
        if i is not None:
            out_real = out_real - turn * (i[first] - i[second])
        out_imag = None
        if want_imag:
            out_imag = turn * (r[first] - r[second])
            if i is not None:
                out_imag = out_imag + cos * (i[first] + i[second])
        return out_real, out_imag

    reals_of = (real0, real1, real2, real3)
    imags_of = (None, imag1, imag2, imag3)

    def term(n, count, where, measure):
        cur_r, cur_i = reals_of[n - 1], imags_of[n - 1]
        complex_in, want_imag, keep_new = n > 1, n < TERMS, n < TERMS

        def row(x, half, measured):
            r8 = pl.ds(half * 8, 8)
            reals = [[cur_r[s, x + d, r8, :] for d in (-1, 0, 1)] for s in range(2)]
            imags = [None, None]
            if complex_in:
                imags = [[cur_i[s, x + d, r8, :] for d in (-1, 0, 1)] for s in range(2)]
            for s, chiral in ((0, 1.0), (1, -1.0)):
                r, i = reals[s], imags[s]
                other_r, other_i = reals[1 - s], imags[1 - s]
                here = bond(r, i, 2, 0, chiral, want_imag)
                behind = bond(r, i, 1, 2, chiral, want_imag)
                front = bond(r, i, 0, 1, chiral, want_imag)
                level = onsite[s, pl.ds(x, 1), :]
                scale = factor[s, pl.ds(x, 1), :]
                if n > 1:
                    level, scale = 2.0 * level, 2.0 * scale
                away = 0 if s == 0 else 2
                results = []
                for part in range(2 if want_imag else 1):
                    own, other = (r, other_r) if part == 0 else (i, other_i)
                    hop, prior, later = here[part], behind[part], front[part]
                    if other is not None:
                        hop = hop - (other[1] + other[away])
                        if s == 0:
                            prior = prior - other[1]
                        else:
                            later = later - other[1]
                    result = (hop + (back(prior) + ahead(later))) * scale
                    if own is not None:
                        result = result + level * own[1]
                    fields = reals_of if part == 0 else imags_of
                    if n > 1 and fields[n - 2] is not None:
                        result = result - fields[n - 2][s, x, r8, :]
                    if keep_new:
                        fields[n][s, x, r8, :] = result
                    results.append(result[:, :long])
                if measured is not None:
                    measured(s, half, real0[s, x, r8, 0:long], results,
                             r[1][:, :long], None if i is None else i[1][:, :long])

        def plain(t, carry):
            x = where(t)
            for half in range(halves):
                row(x, half, None)
            return carry

        def middle(t, carry):
            x = where(t)
            sums = [None, None]

            def measured(s, half, start, results, now_r, now_i):
                product = start * results[0]
                sums[s] = product if sums[s] is None else sums[s] + product
                if n == 1:
                    extra = ((0, product), (4, start * start))
                elif n == 2:
                    extra = (
                        (1, product),
                        (2, now_r * results[0] + now_i * results[1]),
                        (3, results[0] * results[0] + results[1] * results[1]),
                    )
                else:
                    extra = ()
                for place, value in extra:
                    total = traces[place, half * 8 : half * 8 + 8, :]
                    for k in range(long // BLOCK):
                        total = total + value[:, k * BLOCK : (k + 1) * BLOCK]
                    traces[place, half * 8 : half * 8 + 8, :] = total

            for half in range(halves):
                row(x, half, measured)
            for s in range(2):
                moments_ref[n - 1, s, pl.ds(x - HALO, 1), :] = (
                    jnp.sum(sums[s], axis=0, keepdims=True) * (1.0 / vectors))
            return carry

        lax.fori_loop(0, count, middle if measure else plain, 0)

    def inside(n):
        term(n, wide - 2 * n, lambda t: HALO + n + t, True)

    def border(n):
        out = HALO - n
        term(n, 2 * out, lambda t: n + t + wide * (t // out), False)
        term(n, 2 * n, lambda t: HALO + t + (wide - 2 * n) * (t // n), True)

    for way in ((0, 1), (0, -1)):
        halos[way].wait()
    begin(0)
    for n in range(1, TERMS):
        inside(n)
    for way in WAYS:
        if way[0] != 0:
            halos[way].wait()
    begin(-1)
    begin(1)
    border(1)
    border(2)

    slot = lax.broadcasted_iota(jnp.int32, (vectors, BLOCK), 0)
    part[...] = jnp.zeros_like(part)
    for n in range(TERMS):
        value = traces[n]
        if n == 2:
            value = 2.0 * value - traces[0]
        if n == 3:
            value = 2.0 * value - traces[4]
        spread = jnp.where(slot == lane, jnp.sum(value, axis=1, keepdims=True), 0.0)
        part[0, n : n + 1, :] = jnp.sum(spread, axis=0, keepdims=True)

    def scatter(stage, count, me, slots, place):
        slots[me] = part[stage]
        sent = []
        for i in range(1, count):
            move = copy(part.at[stage], slots.at[me], sum_send.at[stage, i],
                        sum_recv.at[stage, i], place(i))
            move.start()
            sent.append(move)
        return sent

    def collect(sent, count, slots):
        for move in sent:
            move.wait()
        total = slots[0]
        for p in range(1, count):
            total = total + slots[p]
        return total

    sent = scatter(0, ny, gy, parts_y, lambda i: at(0, i))
    border(3)
    part[1] = collect(sent, ny, parts_y)
    sent = scatter(1, nx, gx, parts_x, lambda i: at(i, 0))
    term(TERMS, wide, lambda t: HALO + t, True)
    total = collect(sent, nx, parts_x)
    sites_total = 2 * wide * nx * long * ny
    trace_ref[...] = total[:TERMS, :vectors] * (1.0 / sites_total)


def local(nx, ny, stored_vectors, disorder, vacancy, plan):
    vectors, wide, long = stored_vectors.shape[1:]
    tall, extent = wide + 2 * HALO, long + BLOCK
    vmem = pl.BlockSpec(memory_space=pltpu.VMEM)
    bf16, i32 = jnp.bfloat16, jnp.int32
    dma = pltpu.SemaphoreType.DMA
    ways, most = len(WAYS), max(nx, ny)
    return pl.pallas_call(
        functools.partial(program, nx, ny),
        out_shape=(
            jax.ShapeDtypeStruct((TERMS, 2, wide, long), F32),
            jax.ShapeDtypeStruct((TERMS, vectors), F32),
        ),
        in_specs=[pl.BlockSpec(memory_space=pltpu.SMEM), vmem, vmem, vmem],
        out_specs=(vmem,) * 2,
        scratch_shapes=[
            pltpu.VMEM((long // BLOCK, 2, wide, vectors, BLOCK), bf16),
            pltpu.VMEM((ny, 2, wide, vectors, BLOCK), bf16),
            pltpu.VMEM((ny, 2, wide, vectors, BLOCK), bf16),
            pltpu.VMEM((2, tall, vectors, long), bf16),
            pltpu.VMEM((ways, vectors, BLOCK), bf16),
            pltpu.VMEM((ways, 2, wide, long), F32),
            pltpu.VMEM((ways, 2, wide, BLOCK), F32),
            pltpu.VMEM((ways, 2, wide, long), i32),
            pltpu.VMEM((ways, 2, wide, BLOCK), i32),
        ]
        + [pltpu.VMEM((2, tall, extent), F32)] * 3
        + [pltpu.VMEM((2, tall, vectors, extent), F32)] * 7
        + [
            pltpu.VMEM((TERMS + 1, vectors, BLOCK), F32),
            pltpu.VMEM((2, vectors, BLOCK), bf16),
            pltpu.VMEM((2, 8, BLOCK), F32),
            pltpu.VMEM((ny, 8, BLOCK), F32),
            pltpu.VMEM((nx, 8, BLOCK), F32),
            dma((ny,)), dma((ny,)), dma((ways,)), dma((ways,)), dma((ways, 2)), dma((ways, 2)),
            dma((2, most)), dma((2, most)),
        ],
        compiler_params=pltpu.CompilerParams(collective_id=0, has_side_effects=True),
        name="chebyshev",
    )(plan, stored_vectors, disorder, vacancy)


def solution(mesh):
    placed = (P(None, None, "gx", "gy"), P(None, "gx", "gy"), P(None, "gx", "gy"), P())
    return jax.shard_map(
        functools.partial(local, mesh.shape["gx"], mesh.shape["gy"]),
        mesh=mesh,
        in_specs=placed,
        out_specs=(P(None, None, "gx", "gy"), P()),
        check_vma=False,
    )
```

profile of v0, /device:TPU:0, one launch (start us, length us, event | category | flops | bytes accessed | tf_op | source)
XLA Modules:
  0.0 38.8 jit_solution(4419737913986395236)
XLA Ops:
  0.6 36.0 %chebyshev.1 = (f32[4,2,8,512]{3,2,1,0:T(8,128)}, f32[4,16]{1,0:T(4,128)}) custom-call(s32[32]{0:T(128)} %plan_ref.1, bf16[2,16,8,512]{3,2,1,0:T(8,128)(2,1)} %stored_ref.1, f32[2,8,512]{2,1,0:T(8,128)} %disorder_ref.1, s32[2,8,512]{2,1,0:T(8,128)} %vacancy_ref.1), custom_call_target="tpu_custom_call" | custom-call | tf_op jit(solution)/shard_map/chebyshev/pallas_call | solution.py:334
  36.6 0.0 copy-start
  36.6 1.6 %copy.8 = f32[4,2,8,512]{3,2,1,0:T(8,128)} copy(f32[4,2,8,512]{3,2,1,0:T(8,128)} %get-tuple-element.4) | data formatting | bytes 262144
  38.2 0.0 copy-done
  38.2 0.6 %copy.9 = f32[4,16]{1,0:T(4,128)} copy(f32[4,16]{1,0:T(4,128)S(1)} %copy-done) | data formatting | bytes 512
Async XLA Ops:
  36.6 1.6 %copy-start = (f32[4,16]{1,0:T(4,128)S(1)}, f32[4,16]{1,0:T(4,128)}, u32[]{:S(2)}) copy-start(f32[4,16]{1,0:T(4,128)} %get-tuple-element.5) | copy-start | bytes 772
where the time goes:
time: 38.9 us; the launch traced here: 38.8 us
  Pallas kernels  36 us (93%)
  local copies, waits for them, and re-layouts  2.15 us (6%)
  between operations  0.65 us (2%)
    pallas_call x1, Pallas kernels, local(): pl.pallas_call(functools.partial(program, nx, ny), out_shape=(jax.ShapeDt...  36 us
    unnamed x4, local copies, waits for them, and re-layouts  2.15 us

commit v1 on v0

v1 whole, which is shorter than its diff:
```python
import functools

import jax
import jax.numpy as jnp
from jax import lax
from jax.experimental import pallas as pl
from jax.experimental.pallas import tpu as pltpu
from jax.sharding import PartitionSpec as P

BLOCK = 128
TERMS = 4
HOP_NEXT = 0.3
TWIST_COS = 0.4535961214255773
TWIST_SIN = 0.8912073600614354
SPREAD = 6.5
HALO = TERMS
NEAR = 2
GROUP = 8
MESH = pl.DeviceIdType.MESH
F32 = jnp.float32
BF16 = jnp.bfloat16

WAYS = tuple((a, b) for a in (-1, 0, 1) for b in (-1, 0, 1) if (a, b) != (0, 0))


def rows_from(a, wide):
    if a == 0:
        return slice(HALO, HALO + wide)
    return slice(0, HALO) if a == 1 else slice(HALO + wide, 2 * HALO + wide)


def rows_to(a, wide):
    if a == 0:
        return slice(0, wide)
    return slice(wide - HALO, wide) if a == 1 else slice(0, HALO)


def program(
    nx, ny,
    plan_any, stored_any, disorder_any, vacancy_any,
    moments_ref, trace_ref,
    plan_ref, stored_ref, disorder_ref, vacancy_ref,
    turned, strips, send, edge_send, lattice, edge_own, edge_side,
    level_x, vac_x, site_edge, site_y, keep_ref, onsite, factor,
    real0, real1, real2, real3, imag1, imag2, imag3, sums, traces, part, parts,
    load_sem, a2a_send, a2a_recv, halo_send, halo_recv, site_send, site_recv, sum_send, sum_recv,
    *landing,
):
    gx, gy = lax.axis_index("gx"), lax.axis_index("gy")
    wide, long = disorder_ref.shape[1], disorder_ref.shape[2]
    halves = lattice.shape[0]
    vectors = halves * GROUP
    recv, edge_recv = landing[:halves], landing[halves:]
    extent = long + BLOCK
    blocks = long // BLOCK
    many = nx * ny
    cos, sin = HOP_NEXT * TWIST_COS, HOP_NEXT * TWIST_SIN

    def at(a, b):
        return (lax.rem(gx + a + nx, nx), lax.rem(gy + b + ny, ny))

    def copy(source, target, out_sem, in_sem, device):
        return pltpu.make_async_remote_copy(
            src_ref=source, dst_ref=target, send_sem=out_sem, recv_sem=in_sem,
            device_id=device, device_id_type=MESH,
        )

    loads = []
    for t, (source, target) in enumerate((
        (stored_any, stored_ref), (plan_any, plan_ref),
        (disorder_any, disorder_ref), (vacancy_any, vacancy_ref),
    )):
        loads.append(pltpu.make_async_copy(source, target, load_sem.at[t]))
        loads[-1].start()
    barrier = pltpu.get_barrier_semaphore()
    for i in range(1, many):
        pl.semaphore_signal(barrier, inc=1, device_id=at(i // ny, i % ny), device_id_type=MESH)
    traces[...] = jnp.zeros_like(traces)
    for load in loads:
        load.wait()

    lane = lax.broadcasted_iota(jnp.int32, (2 * GROUP, BLOCK), 1)
    place = ((lane + HALO) & (BLOCK - 1)) // (2 * HALO)
    is_last = (lane & HALO) != 0

    def turn(h):
        for k in range(blocks):
            piece = stored_ref[:, h * GROUP : (h + 1) * GROUP, :, k * BLOCK : (k + 1) * BLOCK]
            piece = piece.astype(F32).reshape(2 * GROUP, wide, BLOCK)
            piece = jnp.transpose(piece, (1, 0, 2))
            turned[h, k] = piece.astype(BF16)
            strip = piece[0]
            for x in range(1, wide):
                moved = pltpu.roll(piece[x], 2 * HALO * x, axis=1)
                strip = jnp.where(place == x, moved, strip)
            strips[h, k] = strip

    def mine(index):
        return plan_ref[lax.rem(index + ny * blocks, ny * blocks)] - gy * blocks

    def inside_mine(offset):
        return (offset >= 0) & (offset < blocks)

    picks = []
    for i in range(ny):
        target = lax.rem(gy + i, ny)
        pick = 0
        for j in range(blocks):
            offset = mine(target * blocks + j)
            pick = jnp.where(inside_mine(offset), offset, pick)
        left, right = mine(target * blocks - 1), mine(target * blocks + blocks)
        left = jnp.where(inside_mine(left), left, 0)
        right = jnp.where(inside_mine(right), right, 0)
        picks.append((pick, left, right))

    def fill(h):
        for i in range(1, ny):
            send[h, i] = turned[h, picks[i][0]]
        recv[h][gy] = turned[h, picks[0][0]]

    def fill_edges(h):
        def edge(i):
            return jnp.where(is_last, strips[h, picks[i][1]], strips[h, picks[i][2]]).astype(BF16)
        for i in range(1, ny):
            edge_send[h, i] = edge(i)
        edge_recv[h][gy] = edge(0)

    moves = [[] for _ in range(halves)]

    def start_blocks(h):
        for i in range(1, ny):
            move = copy(send.at[h, i], recv[h].at[gy], a2a_send.at[h, 0, i],
                        a2a_recv.at[h, 0, i], at(0, i))
            move.start()
            moves[h].append(move)

    def start_edges(h):
        for i in range(1, ny):
            move = copy(edge_send.at[h, i], edge_recv[h].at[gy], a2a_send.at[h, 1, i],
                        a2a_recv.at[h, 1, i], at(0, i))
            move.start()
            moves[h].append(move)

    turn(0)
    fill(0)
    fill_edges(0)
    pl.semaphore_wait(barrier, many - 1)
    start_blocks(0)
    start_edges(0)

    site_lane = lax.broadcasted_iota(jnp.int32, (2, wide, BLOCK), 2)
    low = site_lane < BLOCK // 2
    ends = []
    for own in (disorder_ref, vacancy_ref):
        ends.append(jnp.where(low, own[:, :, 0:BLOCK].astype(F32),
                              own[:, :, long - BLOCK : long].astype(F32)))
    shifted = pltpu.roll(ends[1], 4 * HALO, axis=2)
    near_end = ((site_lane + HALO) & (BLOCK - 1)) < 2 * HALO
    site_edge[...] = jnp.where(near_end, ends[0], shifted)
    low_shifted = ((site_lane - 4 * HALO) & (BLOCK - 1)) < BLOCK // 2
    sites = []

    def site_move(source, target, w, t):
        move = copy(source, target, site_send.at[w, t], site_recv.at[w, t], at(*WAYS[w]))
        move.start()
        sites.append(move)

    for w, (a, b) in enumerate(WAYS):
        if b == 0:
            site_move(disorder_ref, level_x.at[0 if a == -1 else 1], w, 0)
            site_move(vacancy_ref, vac_x.at[0 if a == -1 else 1], w, 1)
        else:
            site_move(site_edge, site_y.at[w], w, 0)

    for h in range(1, halves):
        turn(h)
        fill(h)
        start_blocks(h)
        fill_edges(h)
        start_edges(h)

    for move in sites:
        move.wait()
    for a in (-1, 0, 1):
        side = 0 if a == -1 else 1
        level = disorder_ref[...] if a == 0 else level_x[side]
        keep = (vacancy_ref[...] if a == 0 else vac_x[side]).astype(F32)
        right, left = site_y[WAYS.index((a, -1))], site_y[WAYS.index((a, 1))]
        edge = jnp.where(low, right, left)
        keep_edge = jnp.where(low_shifted, right, left)
        keep_edge = pltpu.roll(keep_edge, BLOCK - 4 * HALO, axis=2)
        kept, rows = rows_to(a, wide), rows_from(a, wide)
        for lanes, energy, present in (
            (slice(0, long), level, keep), (slice(long, extent), edge, keep_edge),
        ):
            energy, present = energy[:, kept], present[:, kept]
            scale = present * (1.0 / SPREAD)
            keep_ref[:, rows, lanes] = present
            factor[:, rows, lanes] = scale
            onsite[:, rows, lanes] = energy * scale

    def begin(h, first, last, edges):
        for x in range(first, last):
            rows = lattice[h, x].astype(F32)
            shift = (2 * BLOCK - 2 * HALO * edges[1] - 2 * HALO * (x - first)) % BLOCK
            edge = pltpu.roll(edges[0], shift, axis=1) if shift else edges[0]
            for s in range(2):
                mask = keep_ref[s, x : x + 1, :]
                own = slice(s * GROUP, (s + 1) * GROUP)
                real0[h, s, x, :, 0:long] = rows[own] * mask[:, 0:long]
                real0[h, s, x, :, long:] = edge[own] * mask[:, long:]

    halos = [{} for _ in range(halves)]

    def arrive(h):
        for move in moves[h]:
            move.wait()
        for k in range(blocks):
            source = plan_ref[gy * blocks + k] // blocks
            lattice[h, HALO : HALO + wide, :, k * BLOCK : (k + 1) * BLOCK] = recv[h][source]
        left = plan_ref[lax.rem(gy * blocks - 1 + ny * blocks, ny * blocks)] // blocks
        right = plan_ref[lax.rem(gy * blocks + blocks, ny * blocks)] // blocks
        edge = jnp.where(is_last, edge_recv[h][left].astype(F32), edge_recv[h][right].astype(F32))
        edge_own[h] = edge.astype(BF16)
        for part_of in ("near", "edge", "far"):
            for a in (1, -1):
                side = 0 if a == -1 else 1
                if part_of == "edge":
                    source, target = edge_own.at[h], edge_side.at[h, side]
                    slot = 2
                else:
                    near = part_of == "near"
                    slot = 0 if near else 1
                    if (a == 1) == near:
                        cut = slice(HALO - NEAR, HALO)
                    else:
                        cut = slice(0, NEAR)
                    rows_out, rows_in = rows_to(a, wide).start + HALO, rows_from(a, wide).start
                    source = lattice.at[h, rows_out + cut.start : rows_out + cut.stop]
                    target = lattice.at[h, rows_in + cut.start : rows_in + cut.stop]
                move = copy(source, target, halo_send.at[h, side, slot],
                            halo_recv.at[h, side, slot], at(a, 0))
                move.start()
                halos[h][part_of, a] = move
        begin(h, HALO, HALO + wide, (edge, 0))

    def back(value):
        return pltpu.roll(value, 1, axis=1)

    def ahead(value):
        return pltpu.roll(value, extent - 1, axis=1)

    def bond(r, i, first, second, chiral, want_imag):
        turn = chiral * sin
        out_real = cos * (r[first] + r[second])
        if i is not None:
            out_real = out_real - turn * (i[first] - i[second])
        out_imag = None
        if want_imag:
            out_imag = turn * (r[first] - r[second])
            if i is not None:
                out_imag = out_imag + cos * (i[first] + i[second])
        return out_real, out_imag

    reals_of = (real0, real1, real2, real3)
    imags_of = (None, imag1, imag2, imag3)

    def term(n, h, count, where, measure):
        if count <= 0:
            return
        cur_r, cur_i = reals_of[n - 1], imags_of[n - 1]
        complex_in, want_imag, keep_new = n > 1, n < TERMS, n < TERMS

        def row(x, measured):
            reals = [[cur_r[h, s, x + d] for d in (-1, 0, 1)] for s in range(2)]
            imags = [None, None]
            if complex_in:
                imags = [[cur_i[h, s, x + d] for d in (-1, 0, 1)] for s in range(2)]
            for s, chiral in ((0, 1.0), (1, -1.0)):
                r, i = reals[s], imags[s]
                other_r, other_i = reals[1 - s], imags[1 - s]
                here = bond(r, i, 2, 0, chiral, want_imag)
                behind = bond(r, i, 1, 2, chiral, want_imag)
                front = bond(r, i, 0, 1, chiral, want_imag)
                level = onsite[s, pl.ds(x, 1), :]
                scale = factor[s, pl.ds(x, 1), :]
                if n > 1:
                    level, scale = 2.0 * level, 2.0 * scale
                away = 0 if s == 0 else 2
                results = []
                for part_of in range(2 if want_imag else 1):
                    own, other = (r, other_r) if part_of == 0 else (i, other_i)
                    hop, prior, later = here[part_of], behind[part_of], front[part_of]
                    if other is not None:
                        hop = hop - (other[1] + other[away])
                        if s == 0:
                            prior = prior - other[1]
                        else:
                            later = later - other[1]
                    result = (hop + (back(prior) + ahead(later))) * scale
                    if own is not None:
                        result = result + level * own[1]
                    fields = reals_of if part_of == 0 else imags_of
                    if n > 1 and fields[n - 2] is not None:
                        result = result - fields[n - 2][h, s, x]
                    if keep_new:
                        fields[n][h, s, x] = result
                    results.append(result[:, :long])
                if measured is not None:
                    measured(s, x, real0[h, s, x, :, 0:long], results,
                             r[1][:, :long], None if i is None else i[1][:, :long])

        def plain(t, carry):
            row(where(t), None)
            return carry

        def middle(t, carry):
            def measured(s, x, start, results, now_r, now_i):
                product = start * results[0]
                total = product
                if h > 0:
                    total = sums[n - 1, s, x - HALO] + product
                if h < halves - 1:
                    sums[n - 1, s, x - HALO] = total
                else:
                    moments_ref[n - 1, s, pl.ds(x - HALO, 1), :] = (
                        jnp.sum(total, axis=0, keepdims=True) * (1.0 / vectors))
                if n == 1:
                    extra = ((0, product), (4, start * start))
                elif n == 2:
                    extra = (
                        (1, product),
                        (2, now_r * results[0] + now_i * results[1]),
                        (3, results[0] * results[0] + results[1] * results[1]),
                    )
                else:
                    extra = ()
                for slot, value in extra:
                    total = traces[h, slot]
                    for k in range(blocks):
                        total = total + value[:, k * BLOCK : (k + 1) * BLOCK]
                    traces[h, slot] = total

            row(where(t), measured)
            return carry

        lax.fori_loop(0, count, middle if measure else plain, 0)

    def inside(n, h):
        term(n, h, wide - 2 * n, lambda t: HALO + n + t, True)

    def border(n, h):
        term(n, h, 2 * n, lambda t: HALO + t + (wide - 2 * n) * (t // n), True)

    def halo_edges(h):
        return {a: edge_side[h, 0 if a == -1 else 1].astype(F32) for a in (1, -1)}

    def near_stage(h):
        for part_of in ("near", "edge"):
            for a in (1, -1):
                halos[h][part_of, a].wait()
        edges = halo_edges(h)
        begin(h, HALO - NEAR, HALO, (edges[1], wide - NEAR))
        begin(h, HALO + wide, HALO + wide + NEAR, (edges[-1], 0))
        term(1, h, 2, lambda t: HALO - 1 + t * (wide + 1), False)
        border(1, h)
        border(2, h)

    def far_stage(h):
        for a in (1, -1):
            halos[h]["far", a].wait()
        edges = halo_edges(h)
        begin(h, 0, HALO - NEAR, (edges[1], wide - HALO))
        begin(h, HALO + wide + NEAR, 2 * HALO + wide, (edges[-1], NEAR))
        term(1, h, 4, lambda t: 1 + t + (t // 2) * (wide + 2), False)
        term(2, h, 4, lambda t: 2 + t + (t // 2) * wide, False)
        term(3, h, 2, lambda t: 3 + t * (wide + 1), False)
        border(3, h)
        term(TERMS, h, wide, lambda t: HALO + t, True)

    small = lax.broadcasted_iota(jnp.int32, (GROUP, BLOCK), 1)
    slot_of = lax.broadcasted_iota(jnp.int32, (GROUP, BLOCK), 0)

    def gather_traces(h):
        out = jnp.zeros((GROUP, BLOCK), F32)
        for n in range(TERMS):
            value = traces[h, n]
            if n == 2:
                value = 2.0 * value - traces[h, 0]
            if n == 3:
                value = 2.0 * value - traces[h, 4]
            total = jnp.sum(value, axis=1, keepdims=True)
            out = jnp.where(small == slot_of + (n * vectors + h * GROUP), total, out)
        return jnp.sum(out, axis=0, keepdims=True)

    trace_row = jnp.zeros((1, BLOCK), F32)
    for h in range(halves):
        arrive(h)
        for n in range(1, TERMS):
            inside(n, h)
    for h in range(halves):
        near_stage(h)
        trace_row = trace_row + gather_traces(h)
        if h < halves - 1:
            far_stage(h)
    part[...] = trace_row
    me = gx * ny + gy
    parts[me] = trace_row
    sent = []
    for i in range(1, many):
        move = copy(part, parts.at[me], sum_send.at[i], sum_recv.at[i], at(i // ny, i % ny))
        move.start()
        sent.append(move)
    far_stage(halves - 1)
    for move in sent:
        move.wait()
    total = parts[0]
    for p in range(1, many):
        total = total + parts[p]
    sites_total = 2 * wide * nx * long * ny
    total = total * (1.0 / sites_total)
    for n in range(TERMS):
        turned_row = pltpu.roll(total, BLOCK - n * vectors, axis=1) if n else total
        trace_ref[n : n + 1, :] = turned_row[:, :vectors]


def local(nx, ny, stored_vectors, disorder, vacancy, plan):
    vectors, wide, long = stored_vectors.shape[1:]
    tall, extent = wide + 2 * HALO, long + BLOCK
    halves, blocks, pair = vectors // GROUP, long // BLOCK, 2 * GROUP
    dma = pltpu.SemaphoreType.DMA
    ways, many = len(WAYS), nx * ny
    field = pltpu.VMEM((halves, 2, tall, GROUP, extent), F32)
    return pl.pallas_call(
        functools.partial(program, nx, ny),
        out_shape=(
            pltpu.VMEM((TERMS, 2, wide, long), F32),
            pltpu.VMEM((TERMS, vectors), F32),
        ),
        in_specs=[pl.BlockSpec(memory_space=pl.ANY)] * 4,
        out_specs=(pl.BlockSpec(memory_space=pltpu.VMEM),) * 2,
        scratch_shapes=[
            pltpu.SMEM(plan.shape, jnp.int32),
            pltpu.VMEM(stored_vectors.shape, BF16),
            pltpu.VMEM(disorder.shape, F32),
            pltpu.VMEM(vacancy.shape, jnp.int32),
            pltpu.VMEM((halves, blocks, wide, pair, BLOCK), BF16),
            pltpu.VMEM((halves, blocks, pair, BLOCK), F32),
            pltpu.VMEM((halves, ny, wide, pair, BLOCK), BF16),
            pltpu.VMEM((halves, ny, pair, BLOCK), BF16),
            pltpu.VMEM((halves, tall, pair, long), BF16),
            pltpu.VMEM((halves, pair, BLOCK), BF16),
            pltpu.VMEM((halves, 2, pair, BLOCK), BF16),
            pltpu.VMEM((2, 2, wide, long), F32),
            pltpu.VMEM((2, 2, wide, long), jnp.int32),
            pltpu.VMEM((2, wide, BLOCK), F32),
            pltpu.VMEM((ways, 2, wide, BLOCK), F32),
        ]
        + [pltpu.VMEM((2, tall, extent), F32)] * 3
        + [field] * 7
        + [
            pltpu.VMEM((TERMS, 2, wide, GROUP, long), F32),
            pltpu.VMEM((halves, TERMS + 1, GROUP, BLOCK), F32),
            pltpu.VMEM((1, BLOCK), F32),
            pltpu.VMEM((many, 1, BLOCK), F32),
            dma((4,)),
            dma((halves, 2, ny)), dma((halves, 2, ny)),
            dma((halves, 2, 3)), dma((halves, 2, 3)),
            dma((ways, 2)), dma((ways, 2)),
            dma((many,)), dma((many,)),
        ]
        + [pltpu.VMEM((ny, wide, pair, BLOCK), BF16)] * halves
        + [pltpu.VMEM((ny, pair, BLOCK), BF16)] * halves,
        compiler_params=pltpu.CompilerParams(collective_id=0, has_side_effects=True),
        name="chebyshev",
    )(plan, stored_vectors, disorder, vacancy)


def solution(mesh):
    placed = (P(None, None, "gx", "gy"), P(None, "gx", "gy"), P(None, "gx", "gy"), P())
    return jax.shard_map(
        functools.partial(local, mesh.shape["gx"], mesh.shape["gy"]),
        mesh=mesh,
        in_specs=placed,
        out_specs=(P(None, None, "gx", "gy"), P()),
        check_vma=False,
    )
```

time: 38.9 us -> 32.2 us (0.83)
  Pallas kernels: 36 us -> 30.2 us
  local copies, waits for them, and re-layouts: 2.15 us -> 1.24 us
    pallas_call x1, Pallas kernels: 36 us -> 30.2 us  [local(): pl.pallas_call(functools.partial(program, nx, ny), out_shape=(pltpu.VMEM(...]
    unnamed x4 -> x2, local copies, waits for them, and re-layouts: 2.15 us -> 1.24 us
where the time goes in v1:
time: 32.2 us; the launch traced here: 32 us
  Pallas kernels  30.2 us (94%)
  local copies, waits for them, and re-layouts  1.24 us (4%)
  between operations  0.64 us (2%)
    pallas_call x1, Pallas kernels, local(): pl.pallas_call(functools.partial(program, nx, ny), out_shape=(pltpu.VMEM(...  30.2 us
    unnamed x2, local copies, waits for them, and re-layouts  1.24 us

profile of v1, /device:TPU:0, one launch (start us, length us, event | category | flops | bytes accessed | tf_op | source)
XLA Modules:
  0.0 32.0 jit_solution(11204031139871007552)
XLA Ops:
  0.6 30.2 %chebyshev.1 = (f32[4,2,8,512]{3,2,1,0:T(8,128)S(1)}, f32[4,16]{1,0:T(4,128)S(1)}) custom-call(s32[32]{0:T(128)} %plan_any.1, bf16[2,16,8,512]{3,2,1,0:T(8,128)(2,1)} %stored_any.1, f32[2,8,512]{2,1,0:T(8,128)} %disorder_any.1, s32[2,8,512]{2,1,0:T(8,128)} %vacancy_any.1), custom_call_target="tpu_custom_call" | custom-call | tf_op jit(solution)/shard_map/chebyshev/pallas_call | solution.py:434
  30.8 0.7 %copy.8 = f32[4,2,8,512]{3,2,1,0:T(8,128)} copy(f32[4,2,8,512]{3,2,1,0:T(8,128)S(1)} %get-tuple-element.2) | data formatting | bytes 262144
  31.5 0.6 %copy.9 = f32[4,16]{1,0:T(4,128)} copy(f32[4,16]{1,0:T(4,128)S(1)} %get-tuple-element.3) | data formatting | bytes 512

commit v2 on v1

--- a/solution.py
+++ b/solution.py
@@ -20,9 +20,6 @@
 F32 = jnp.float32
 BF16 = jnp.bfloat16
 
-WAYS = tuple((a, b) for a in (-1, 0, 1) for b in (-1, 0, 1) if (a, b) != (0, 0))
-
-
 def rows_from(a, wide):
     if a == 0:
         return slice(HALO, HALO + wide)
@@ -40,8 +37,8 @@
     plan_any, stored_any, disorder_any, vacancy_any,
     moments_ref, trace_ref,
     plan_ref, stored_ref, disorder_ref, vacancy_ref,
-    turned, strips, send, edge_send, lattice, edge_own, edge_side,
-    level_x, vac_x, site_edge, site_y, keep_ref, onsite, factor,
+    turned, strips, send, edge_send, edge_recv, lattice, edge_own, edge_side,
+    site_send_x, site_x, site_edge, site_y, site_both, site_z, keep_ref, onsite, factor,
     real0, real1, real2, real3, imag1, imag2, imag3, sums, traces, part, parts,
     load_sem, a2a_send, a2a_recv, halo_send, halo_recv, site_send, site_recv, sum_send, sum_recv,
     *landing,
@@ -50,7 +47,7 @@
     wide, long = disorder_ref.shape[1], disorder_ref.shape[2]
     halves = lattice.shape[0]
     vectors = halves * GROUP
-    recv, edge_recv = landing[:halves], landing[halves:]
+    recv = landing
     extent = long + BLOCK
     blocks = long // BLOCK
     many = nx * ny
@@ -58,6 +55,19 @@
 
     def at(a, b):
         return (lax.rem(gx + a + nx, nx), lax.rem(gy + b + ny, ny))
+
+    cores = 2 if ny % 2 == 0 else 1
+    cols = 2 if (ny // cores) % 2 == 0 else 1
+    lines = ny // (cores * cols)
+    steps = [(r, c, u) for r in range(lines) for c in range(cols) for u in range(cores)]
+    steps.sort(key=lambda step: -((step[0] != 0) + (step[1] != 0)))
+    steps = [(0, 0, 0)] + [step for step in steps if step != (0, 0, 0)]
+
+    def peer(i):
+        r, c, u = steps[i]
+        line = lax.rem(gy // (cores * cols) + r, lines)
+        col = lax.rem(lax.rem(gy // cores, cols) + c, cols)
+        return (line * cols + col) * cores + lax.rem(lax.rem(gy, cores) + u, cores)
 
     def copy(source, target, out_sem, in_sem, device):
         return pltpu.make_async_remote_copy(
@@ -73,8 +83,10 @@
         loads.append(pltpu.make_async_copy(source, target, load_sem.at[t]))
         loads[-1].start()
     barrier = pltpu.get_barrier_semaphore()
-    for i in range(1, many):
-        pl.semaphore_signal(barrier, inc=1, device_id=at(i // ny, i % ny), device_id_type=MESH)
+    greeted = [(0, b) for b in range(1, ny)] + [(1, 0), (nx - 1, 0)]
+    greeted += [(a, b) for a in range(3, nx - 2) for b in range(ny)]
+    for a, b in greeted:
+        pl.semaphore_signal(barrier, inc=1, device_id=at(a, b), device_id_type=MESH)
     traces[...] = jnp.zeros_like(traces)
     for load in loads:
         load.wait()
@@ -89,11 +101,12 @@
             piece = piece.astype(F32).reshape(2 * GROUP, wide, BLOCK)
             piece = jnp.transpose(piece, (1, 0, 2))
             turned[h, k] = piece.astype(BF16)
-            strip = piece[0]
-            for x in range(1, wide):
-                moved = pltpu.roll(piece[x], 2 * HALO * x, axis=1)
-                strip = jnp.where(place == x, moved, strip)
-            strips[h, k] = strip
+            strip = strips[k] if h else piece[0]
+            for x in range(0 if h else 1, wide):
+                spot = h * wide + x
+                moved = pltpu.roll(piece[x], 2 * HALO * spot, axis=1)
+                strip = jnp.where(place == spot, moved, strip)
+            strips[k] = strip
 
     def mine(index):
         return plan_ref[lax.rem(index + ny * blocks, ny * blocks)] - gy * blocks
@@ -103,7 +116,7 @@
 
     picks = []
     for i in range(ny):
-        target = lax.rem(gy + i, ny)
+        target = peer(i)
         pick = 0
         for j in range(blocks):
             offset = mine(target * blocks + j)
@@ -118,91 +131,113 @@
             send[h, i] = turned[h, picks[i][0]]
         recv[h][gy] = turned[h, picks[0][0]]
 
-    def fill_edges(h):
+    def fill_edges():
         def edge(i):
-            return jnp.where(is_last, strips[h, picks[i][1]], strips[h, picks[i][2]]).astype(BF16)
+            return jnp.where(is_last, strips[picks[i][1]], strips[picks[i][2]]).astype(BF16)
         for i in range(1, ny):
-            edge_send[h, i] = edge(i)
-        edge_recv[h][gy] = edge(0)
+            edge_send[i] = edge(i)
+        edge_recv[gy] = edge(0)
 
     moves = [[] for _ in range(halves)]
 
     def start_blocks(h):
         for i in range(1, ny):
-            move = copy(send.at[h, i], recv[h].at[gy], a2a_send.at[h, 0, i],
-                        a2a_recv.at[h, 0, i], at(0, i))
+            move = copy(send.at[h, i], recv[h].at[gy], a2a_send.at[h, i],
+                        a2a_recv.at[h, i], (gx, peer(i)))
             move.start()
             moves[h].append(move)
 
-    def start_edges(h):
+    def start_edges():
         for i in range(1, ny):
-            move = copy(edge_send.at[h, i], edge_recv[h].at[gy], a2a_send.at[h, 1, i],
-                        a2a_recv.at[h, 1, i], at(0, i))
+            move = copy(edge_send.at[i], edge_recv.at[gy], a2a_send.at[halves, i],
+                        a2a_recv.at[halves, i], (gx, peer(i)))
             move.start()
-            moves[h].append(move)
+            moves[0].append(move)
 
     turn(0)
     fill(0)
-    fill_edges(0)
-    pl.semaphore_wait(barrier, many - 1)
+    site_lane = lax.broadcasted_iota(jnp.int32, (2, wide, BLOCK), 2)
+    site_row = lax.broadcasted_iota(jnp.int32, (2, wide, BLOCK), 1)
+    span = 4 * HALO
+    low = site_lane < BLOCK // 2
+    keep_own = vacancy_ref[...].astype(F32)
+    ends = []
+    for own in (disorder_ref[...], keep_own):
+        ends.append(jnp.where(low, own[:, :, 0:BLOCK], own[:, :, long - BLOCK : long]))
+    keep_end = jnp.where(low, pltpu.roll(ends[1], HALO, axis=2),
+                         pltpu.roll(ends[1], BLOCK - HALO, axis=2))
+    packed = jnp.where(((site_lane + HALO) & (BLOCK - 1)) < 2 * HALO, ends[0], keep_end)
+    packed = pltpu.roll(packed, 0, axis=2, stride=span, stride_axis=1)
+    packed = jnp.where(((site_lane + span // 2) & (BLOCK - 1)) // span == site_row, packed, 0.0)
+    site_edge[...] = jnp.sum(packed, axis=1, keepdims=True)
+    for a in (-1, 1):
+        kept = rows_to(a, wide)
+        rows = (disorder_ref[:, kept, :], keep_own[:, kept, :])
+        site_send_x[0 if a == -1 else 1] = jnp.concatenate(rows, axis=1)
+    sites = {}
+
+    def site(name, source, target, w, device):
+        sites[name] = copy(source, target, site_send.at[w], site_recv.at[w], device)
+        sites[name].start()
+
+    pl.semaphore_wait(barrier, len(greeted))
+    for side, a in enumerate((-1, 1)):
+        site(("x", a), site_send_x.at[side], site_x.at[side], side, at(a, 0))
+        site(("y", a), site_edge, site_y.at[side], 2 + side, at(0, a))
     start_blocks(0)
-    start_edges(0)
-
-    site_lane = lax.broadcasted_iota(jnp.int32, (2, wide, BLOCK), 2)
-    low = site_lane < BLOCK // 2
-    ends = []
-    for own in (disorder_ref, vacancy_ref):
-        ends.append(jnp.where(low, own[:, :, 0:BLOCK].astype(F32),
-                              own[:, :, long - BLOCK : long].astype(F32)))
-    shifted = pltpu.roll(ends[1], 4 * HALO, axis=2)
-    near_end = ((site_lane + HALO) & (BLOCK - 1)) < 2 * HALO
-    site_edge[...] = jnp.where(near_end, ends[0], shifted)
-    low_shifted = ((site_lane - 4 * HALO) & (BLOCK - 1)) < BLOCK // 2
-    sites = []
-
-    def site_move(source, target, w, t):
-        move = copy(source, target, site_send.at[w, t], site_recv.at[w, t], at(*WAYS[w]))
-        move.start()
-        sites.append(move)
-
-    for w, (a, b) in enumerate(WAYS):
-        if b == 0:
-            site_move(disorder_ref, level_x.at[0 if a == -1 else 1], w, 0)
-            site_move(vacancy_ref, vac_x.at[0 if a == -1 else 1], w, 1)
-        else:
-            site_move(site_edge, site_y.at[w], w, 0)
 
     for h in range(1, halves):
         turn(h)
+    fill_edges()
+    start_edges()
+    for h in range(1, halves):
         fill(h)
+        for move in moves[h - 1][: ny - 1]:
+            move.wait_send()
         start_blocks(h)
-        fill_edges(h)
-        start_edges(h)
-
-    for move in sites:
-        move.wait()
-    for a in (-1, 0, 1):
-        side = 0 if a == -1 else 1
-        level = disorder_ref[...] if a == 0 else level_x[side]
-        keep = (vacancy_ref[...] if a == 0 else vac_x[side]).astype(F32)
-        right, left = site_y[WAYS.index((a, -1))], site_y[WAYS.index((a, 1))]
-        edge = jnp.where(low, right, left)
-        keep_edge = jnp.where(low_shifted, right, left)
-        keep_edge = pltpu.roll(keep_edge, BLOCK - 4 * HALO, axis=2)
-        kept, rows = rows_to(a, wide), rows_from(a, wide)
-        for lanes, energy, present in (
-            (slice(0, long), level, keep), (slice(long, extent), edge, keep_edge),
-        ):
-            energy, present = energy[:, kept], present[:, kept]
+
+    short = lax.broadcasted_iota(jnp.int32, (2, 1, BLOCK), 2)
+
+    def site_ends(a, both):
+        rows, kept = rows_from(a, wide), rows_to(a, wide)
+        for x in range(rows.start, rows.stop):
+            shift = 2 * BLOCK - span * (x - rows.start + kept.start)
+            energy = pltpu.roll(both, shift % BLOCK, axis=2)
+            present = jnp.where(short < BLOCK // 2,
+                                pltpu.roll(both, (shift - HALO) % BLOCK, axis=2),
+                                pltpu.roll(both, (shift + HALO) % BLOCK, axis=2))
             scale = present * (1.0 / SPREAD)
-            keep_ref[:, rows, lanes] = present
-            factor[:, rows, lanes] = scale
-            onsite[:, rows, lanes] = energy * scale
+            keep_ref[:, x : x + 1, long:] = present
+            factor[:, x : x + 1, long:] = scale
+            onsite[:, x : x + 1, long:] = energy * scale
+
+    def site_rows(a, energy, present):
+        rows = rows_from(a, wide)
+        scale = present * (1.0 / SPREAD)
+        keep_ref[:, rows, 0:long] = present
+        factor[:, rows, 0:long] = scale
+        onsite[:, rows, 0:long] = energy * scale
+
+    site_rows(0, disorder_ref[...], keep_own)
+    for a in (-1, 1):
+        sites["y", a].wait()
+    site_both[...] = jnp.where((short & (span // 2)) == 0, site_y[0], site_y[1])
+    for side, a in enumerate((-1, 1)):
+        site(("z", a), site_both, site_z.at[side], 4 + side, at(a, 0))
+    site_ends(0, site_both[...])
+    for side, a in enumerate((-1, 1)):
+        sites["x", a].wait()
+        site_rows(a, site_x[side, :, 0:HALO], site_x[side, :, HALO:])
+
+    def far_sites():
+        for side, a in enumerate((-1, 1)):
+            sites["z", a].wait()
+            site_ends(a, site_z[side])
 
     def begin(h, first, last, edges):
         for x in range(first, last):
             rows = lattice[h, x].astype(F32)
-            shift = (2 * BLOCK - 2 * HALO * edges[1] - 2 * HALO * (x - first)) % BLOCK
+            shift = (-2 * HALO * (h * wide + edges[1] + x - first)) % BLOCK
             edge = pltpu.roll(edges[0], shift, axis=1) if shift else edges[0]
             for s in range(2):
                 mask = keep_ref[s, x : x + 1, :]
@@ -212,37 +247,38 @@
 
     halos = [{} for _ in range(halves)]
 
+    def halo(h, name, a, source, target, slot):
+        side = 0 if a == -1 else 1
+        halos[h][name, a] = copy(source, target, halo_send.at[h, side, slot],
+                                 halo_recv.at[h, side, slot], at(a, 0))
+        halos[h][name, a].start()
+
+    def own_edge():
+        left = plan_ref[lax.rem(gy * blocks - 1 + ny * blocks, ny * blocks)] // blocks
+        right = plan_ref[lax.rem(gy * blocks + blocks, ny * blocks)] // blocks
+        return jnp.where(is_last, edge_recv[left].astype(F32), edge_recv[right].astype(F32))
+
     def arrive(h):
-        for move in moves[h]:
-            move.wait()
+        for j, move in enumerate(moves[h]):
+            move.wait_recv()
+            if h == halves - 1 or j >= ny - 1:
+                move.wait_send()
         for k in range(blocks):
             source = plan_ref[gy * blocks + k] // blocks
             lattice[h, HALO : HALO + wide, :, k * BLOCK : (k + 1) * BLOCK] = recv[h][source]
-        left = plan_ref[lax.rem(gy * blocks - 1 + ny * blocks, ny * blocks)] // blocks
-        right = plan_ref[lax.rem(gy * blocks + blocks, ny * blocks)] // blocks
-        edge = jnp.where(is_last, edge_recv[h][left].astype(F32), edge_recv[h][right].astype(F32))
-        edge_own[h] = edge.astype(BF16)
-        for part_of in ("near", "edge", "far"):
+        for name in ("near", "far"):
             for a in (1, -1):
-                side = 0 if a == -1 else 1
-                if part_of == "edge":
-                    source, target = edge_own.at[h], edge_side.at[h, side]
-                    slot = 2
-                else:
-                    near = part_of == "near"
-                    slot = 0 if near else 1
-                    if (a == 1) == near:
-                        cut = slice(HALO - NEAR, HALO)
-                    else:
-                        cut = slice(0, NEAR)
-                    rows_out, rows_in = rows_to(a, wide).start + HALO, rows_from(a, wide).start
-                    source = lattice.at[h, rows_out + cut.start : rows_out + cut.stop]
-                    target = lattice.at[h, rows_in + cut.start : rows_in + cut.stop]
-                move = copy(source, target, halo_send.at[h, side, slot],
-                            halo_recv.at[h, side, slot], at(a, 0))
-                move.start()
-                halos[h][part_of, a] = move
-        begin(h, HALO, HALO + wide, (edge, 0))
+                last = (a == 1) == (name == "near")
+                cut = slice(HALO - NEAR, HALO) if last else slice(0, NEAR)
+                rows_out, rows_in = rows_to(a, wide).start + HALO, rows_from(a, wide).start
+                source = lattice.at[h, rows_out + cut.start : rows_out + cut.stop]
+                target = lattice.at[h, rows_in + cut.start : rows_in + cut.stop]
+                halo(h, name, a, source, target, 0 if name == "near" else 1)
+            if h == 0 and name == "near":
+                edge_own[...] = own_edge().astype(BF16)
+                for a in (1, -1):
+                    halo(0, "edge", a, edge_own, edge_side.at[0 if a == -1 else 1], 2)
+        begin(h, HALO, HALO + wide, (own_edge(), 0))
 
     def back(value):
         return pltpu.roll(value, 1, axis=1)
@@ -352,14 +388,15 @@
     def border(n, h):
         term(n, h, 2 * n, lambda t: HALO + t + (wide - 2 * n) * (t // n), True)
 
-    def halo_edges(h):
-        return {a: edge_side[h, 0 if a == -1 else 1].astype(F32) for a in (1, -1)}
+    def halo_edges():
+        return {a: edge_side[0 if a == -1 else 1].astype(F32) for a in (1, -1)}
 
     def near_stage(h):
-        for part_of in ("near", "edge"):
-            for a in (1, -1):
-                halos[h][part_of, a].wait()
-        edges = halo_edges(h)
+        for a in (1, -1):
+            if h == 0:
+                halos[h]["edge", a].wait()
+            halos[h]["near", a].wait()
+        edges = halo_edges()
         begin(h, HALO - NEAR, HALO, (edges[1], wide - NEAR))
         begin(h, HALO + wide, HALO + wide + NEAR, (edges[-1], 0))
         term(1, h, 2, lambda t: HALO - 1 + t * (wide + 1), False)
@@ -369,7 +406,7 @@
     def far_stage(h):
         for a in (1, -1):
             halos[h]["far", a].wait()
-        edges = halo_edges(h)
+        edges = halo_edges()
         begin(h, 0, HALO - NEAR, (edges[1], wide - HALO))
         begin(h, HALO + wide + NEAR, 2 * HALO + wide, (edges[-1], NEAR))
         term(1, h, 4, lambda t: 1 + t + (t // 2) * (wide + 2), False)
@@ -398,11 +435,10 @@
         arrive(h)
         for n in range(1, TERMS):
             inside(n, h)
+    far_sites()
     for h in range(halves):
         near_stage(h)
         trace_row = trace_row + gather_traces(h)
-        if h < halves - 1:
-            far_stage(h)
     part[...] = trace_row
     me = gx * ny + gy
     parts[me] = trace_row
@@ -411,7 +447,8 @@
         move = copy(part, parts.at[me], sum_send.at[i], sum_recv.at[i], at(i // ny, i % ny))
         move.start()
         sent.append(move)
-    far_stage(halves - 1)
+    for h in range(halves):
+        far_stage(h)
     for move in sent:
         move.wait()
     total = parts[0]
@@ -429,7 +466,7 @@
     tall, extent = wide + 2 * HALO, long + BLOCK
     halves, blocks, pair = vectors // GROUP, long // BLOCK, 2 * GROUP
     dma = pltpu.SemaphoreType.DMA
-    ways, many = len(WAYS), nx * ny
+    many = nx * ny
     field = pltpu.VMEM((halves, 2, tall, GROUP, extent), F32)
     return pl.pallas_call(
         functools.partial(program, nx, ny),
@@ -445,16 +482,19 @@
             pltpu.VMEM(disorder.shape, F32),
             pltpu.VMEM(vacancy.shape, jnp.int32),
             pltpu.VMEM((halves, blocks, wide, pair, BLOCK), BF16),
-            pltpu.VMEM((halves, blocks, pair, BLOCK), F32),
+            pltpu.VMEM((blocks, pair, BLOCK), F32),
             pltpu.VMEM((halves, ny, wide, pair, BLOCK), BF16),
-            pltpu.VMEM((halves, ny, pair, BLOCK), BF16),
+            pltpu.VMEM((ny, pair, BLOCK), BF16),
+            pltpu.VMEM((ny, pair, BLOCK), BF16),
             pltpu.VMEM((halves, tall, pair, long), BF16),
-            pltpu.VMEM((halves, pair, BLOCK), BF16),
-            pltpu.VMEM((halves, 2, pair, BLOCK), BF16),
-            pltpu.VMEM((2, 2, wide, long), F32),
-            pltpu.VMEM((2, 2, wide, long), jnp.int32),
-            pltpu.VMEM((2, wide, BLOCK), F32),
-            pltpu.VMEM((ways, 2, wide, BLOCK), F32),
+            pltpu.VMEM((pair, BLOCK), BF16),
+            pltpu.VMEM((2, pair, BLOCK), BF16),
+            pltpu.VMEM((2, 2, 2 * HALO, long), F32),
+            pltpu.VMEM((2, 2, 2 * HALO, long), F32),
+            pltpu.VMEM((2, 1, BLOCK), F32),
+            pltpu.VMEM((2, 2, 1, BLOCK), F32),
+            pltpu.VMEM((2, 1, BLOCK), F32),
+            pltpu.VMEM((2, 2, 1, BLOCK), F32),
         ]
         + [pltpu.VMEM((2, tall, extent), F32)] * 3
         + [field] * 7
@@ -464,13 +504,12 @@
             pltpu.VMEM((1, BLOCK), F32),
             pltpu.VMEM((many, 1, BLOCK), F32),
             dma((4,)),
-            dma((halves, 2, ny)), dma((halves, 2, ny)),
+            dma((halves + 1, ny)), dma((halves + 1, ny)),
             dma((halves, 2, 3)), dma((halves, 2, 3)),
-            dma((ways, 2)), dma((ways, 2)),
+            dma((6,)), dma((6,)),
             dma((many,)), dma((many,)),
         ]
-        + [pltpu.VMEM((ny, wide, pair, BLOCK), BF16)] * halves
-        + [pltpu.VMEM((ny, pair, BLOCK), BF16)] * halves,
+        + [pltpu.VMEM((ny, wide, pair, BLOCK), BF16)] * halves,
         compiler_params=pltpu.CompilerParams(collective_id=0, has_side_effects=True),
         name="chebyshev",
     )(plan, stored_vectors, disorder, vacancy)

time: 32.2 us -> 29.2 us (0.907)
  Pallas kernels: 30.2 us -> 27.1 us
    pallas_call x1, Pallas kernels: 30.2 us -> 27.1 us  [local(): pl.pallas_call(functools.partial(program, nx, ny), out_shape=(pltpu.VMEM(...]
where the time goes in v2:
time: 29.2 us; the launch traced here: 29 us
  Pallas kernels  27.1 us (93%)
  local copies, waits for them, and re-layouts  1.24 us (4%)
  between operations  0.64 us (2%)
    pallas_call x1, Pallas kernels, local(): pl.pallas_call(functools.partial(program, nx, ny), out_shape=(pltpu.VMEM(...  27.1 us
    unnamed x2, local copies, waits for them, and re-layouts  1.24 us

profile of v2, /device:TPU:0, one launch (start us, length us, event | category | flops | bytes accessed | tf_op | source)
XLA Modules:
  0.0 29.0 jit_solution(3634924299040150818)
XLA Ops:
  0.6 27.1 %chebyshev.1 = (f32[4,2,8,512]{3,2,1,0:T(8,128)S(1)}, f32[4,16]{1,0:T(4,128)S(1)}) custom-call(s32[32]{0:T(128)} %plan_any.1, bf16[2,16,8,512]{3,2,1,0:T(8,128)(2,1)} %stored_any.1, f32[2,8,512]{2,1,0:T(8,128)} %disorder_any.1, s32[2,8,512]{2,1,0:T(8,128)} %vacancy_any.1), custom_call_target="tpu_custom_call" | custom-call | tf_op jit(solution)/shard_map/chebyshev/pallas_call | solution.py:471
  27.8 0.7 %copy.8 = f32[4,2,8,512]{3,2,1,0:T(8,128)} copy(f32[4,2,8,512]{3,2,1,0:T(8,128)S(1)} %get-tuple-element.2) | data formatting | bytes 262144
  28.4 0.6 %copy.9 = f32[4,16]{1,0:T(4,128)} copy(f32[4,16]{1,0:T(4,128)S(1)} %get-tuple-element.3) | data formatting | bytes 512

commit v3 on v2

--- a/solution.py
+++ b/solution.py
@@ -40,7 +40,7 @@
     turned, strips, send, edge_send, edge_recv, lattice, edge_own, edge_side,
     site_send_x, site_x, site_edge, site_y, site_both, site_z, keep_ref, onsite, factor,
     real0, real1, real2, real3, imag1, imag2, imag3, sums, traces, part, parts,
-    load_sem, a2a_send, a2a_recv, halo_send, halo_recv, site_send, site_recv, sum_send, sum_recv,
+    load_sem, a2a_send, a2a_recv, halo_send, halo_recv, site_send, site_recv, sum_send, sum_recv, token,
     *landing,
 ):
     gx, gy = lax.axis_index("gx"), lax.axis_index("gy")
@@ -83,10 +83,25 @@
         loads.append(pltpu.make_async_copy(source, target, load_sem.at[t]))
         loads[-1].start()
     barrier = pltpu.get_barrier_semaphore()
-    greeted = [(0, b) for b in range(1, ny)] + [(1, 0), (nx - 1, 0)]
-    greeted += [(a, b) for a in range(3, nx - 2) for b in range(ny)]
-    for a, b in greeted:
-        pl.semaphore_signal(barrier, inc=1, device_id=at(a, b), device_id_type=MESH)
+    linked = {-1: gx > 0, 1: gx < nx - 1}
+
+    def greet(sem, a, b):
+        pl.semaphore_signal(sem, inc=1, device_id=at(a, b), device_id_type=MESH)
+
+    for b in range(1, ny):
+        greet(barrier, 0, b)
+    for a in (-1, 1):
+        pl.when(linked[a])(functools.partial(greet, barrier, a, 0))
+    entered = ny - 1 + linked[-1].astype(jnp.int32) + linked[1].astype(jnp.int32)
+
+    def pass_on(step):
+        for side, a in enumerate((-1, 1)):
+            pl.when(linked[a])(functools.partial(greet, token.at[step, 1 - side], a, 0))
+
+    def hear(step):
+        for side, a in enumerate((-1, 1)):
+            pl.when(linked[a])(functools.partial(pl.semaphore_wait, token.at[step, side], 1))
+
     traces[...] = jnp.zeros_like(traces)
     for load in loads:
         load.wait()
@@ -176,13 +191,17 @@
         site_send_x[0 if a == -1 else 1] = jnp.concatenate(rows, axis=1)
     sites = {}
 
-    def site(name, source, target, w, device):
+    def site(name, source, target, w, device, when=None):
         sites[name] = copy(source, target, site_send.at[w], site_recv.at[w], device)
-        sites[name].start()
-
-    pl.semaphore_wait(barrier, len(greeted))
+        if when is None:
+            sites[name].start()
+        else:
+            pl.when(when)(sites[name].start)
+
+    pl.semaphore_wait(barrier, entered)
+    pass_on(0)
     for side, a in enumerate((-1, 1)):
-        site(("x", a), site_send_x.at[side], site_x.at[side], side, at(a, 0))
+        site(("x", a), site_send_x.at[side], site_x.at[side], side, at(a, 0), linked[a])
         site(("y", a), site_edge, site_y.at[side], 2 + side, at(0, a))
     start_blocks(0)
 
@@ -190,11 +209,21 @@
         turn(h)
     fill_edges()
     start_edges()
+    def token_round(step):
+        hear(step)
+        if step < nx - 3:
+            pass_on(step + 1)
+
+    for step in range(nx - 3):
+        token_round(step)
     for h in range(1, halves):
         fill(h)
         for move in moves[h - 1][: ny - 1]:
             move.wait_send()
         start_blocks(h)
+    token_round(nx - 3)
+    for a in (-1, 1):
+        pl.when(~linked[a])(sites["x", a].start)
 
     short = lax.broadcasted_iota(jnp.int32, (2, 1, BLOCK), 2)
 
@@ -225,12 +254,11 @@
     for side, a in enumerate((-1, 1)):
         site(("z", a), site_both, site_z.at[side], 4 + side, at(a, 0))
     site_ends(0, site_both[...])
-    for side, a in enumerate((-1, 1)):
-        sites["x", a].wait()
-        site_rows(a, site_x[side, :, 0:HALO], site_x[side, :, HALO:])
 
     def far_sites():
         for side, a in enumerate((-1, 1)):
+            sites["x", a].wait()
+            site_rows(a, site_x[side, :, 0:HALO], site_x[side, :, HALO:])
             sites["z", a].wait()
             site_ends(a, site_z[side])
 
@@ -258,6 +286,15 @@
         right = plan_ref[lax.rem(gy * blocks + blocks, ny * blocks)] // blocks
         return jnp.where(is_last, edge_recv[left].astype(F32), edge_recv[right].astype(F32))
 
+    def send_rows(h, name):
+        for a in (1, -1):
+            last = (a == 1) == (name == "near")
+            cut = slice(HALO - NEAR, HALO) if last else slice(0, NEAR)
+            rows_out, rows_in = rows_to(a, wide).start + HALO, rows_from(a, wide).start
+            source = lattice.at[h, rows_out + cut.start : rows_out + cut.stop]
+            target = lattice.at[h, rows_in + cut.start : rows_in + cut.stop]
+            halo(h, name, a, source, target, 0 if name == "near" else 1)
+
     def arrive(h):
         for j, move in enumerate(moves[h]):
             move.wait_recv()
@@ -266,18 +303,11 @@
         for k in range(blocks):
             source = plan_ref[gy * blocks + k] // blocks
             lattice[h, HALO : HALO + wide, :, k * BLOCK : (k + 1) * BLOCK] = recv[h][source]
-        for name in ("near", "far"):
+        send_rows(h, "near")
+        if h == 0:
+            edge_own[...] = own_edge().astype(BF16)
             for a in (1, -1):
-                last = (a == 1) == (name == "near")
-                cut = slice(HALO - NEAR, HALO) if last else slice(0, NEAR)
-                rows_out, rows_in = rows_to(a, wide).start + HALO, rows_from(a, wide).start
-                source = lattice.at[h, rows_out + cut.start : rows_out + cut.stop]
-                target = lattice.at[h, rows_in + cut.start : rows_in + cut.stop]
-                halo(h, name, a, source, target, 0 if name == "near" else 1)
-            if h == 0 and name == "near":
-                edge_own[...] = own_edge().astype(BF16)
-                for a in (1, -1):
-                    halo(0, "edge", a, edge_own, edge_side.at[0 if a == -1 else 1], 2)
+                halo(0, "edge", a, edge_own, edge_side.at[0 if a == -1 else 1], 2)
         begin(h, HALO, HALO + wide, (own_edge(), 0))
 
     def back(value):
@@ -380,7 +410,7 @@
             row(where(t), measured)
             return carry
 
-        lax.fori_loop(0, count, middle if measure else plain, 0)
+        lax.fori_loop(0, count, middle if measure else plain, 0, unroll=True)
 
     def inside(n, h):
         term(n, h, wide - 2 * n, lambda t: HALO + n + t, True)
@@ -395,7 +425,9 @@
         for a in (1, -1):
             if h == 0:
                 halos[h]["edge", a].wait()
-            halos[h]["near", a].wait()
+            halos[h]["near", a].wait_recv()
+            if h < halves - 1:
+                halos[h]["near", a].wait_send()
         edges = halo_edges()
         begin(h, HALO - NEAR, HALO, (edges[1], wide - NEAR))
         begin(h, HALO + wide, HALO + wide + NEAR, (edges[-1], 0))
@@ -436,6 +468,10 @@
         for n in range(1, TERMS):
             inside(n, h)
     far_sites()
+    for a in (1, -1):
+        halos[halves - 1]["near", a].wait_send()
+    for h in range(halves):
+        send_rows(h, "far")
     for h in range(halves):
         near_stage(h)
         trace_row = trace_row + gather_traces(h)
@@ -508,6 +544,7 @@
             dma((halves, 2, 3)), dma((halves, 2, 3)),
             dma((6,)), dma((6,)),
             dma((many,)), dma((many,)),
+            pltpu.SemaphoreType.REGULAR((nx - 2, 2)),
         ]
         + [pltpu.VMEM((ny, wide, pair, BLOCK), BF16)] * halves,
         compiler_params=pltpu.CompilerParams(collective_id=0, has_side_effects=True),

time: 29.2 us -> 25.2 us (0.86)
  Pallas kernels: 27.1 us -> 23.2 us
    pallas_call x1, Pallas kernels: 27.1 us -> 23.2 us  [local(): pl.pallas_call(functools.partial(program, nx, ny), out_shape=(pltpu.VMEM(...]
where the time goes in v3:
time: 25.2 us; the launch traced here: 25.1 us
  Pallas kernels  23.2 us (92%)
  local copies, waits for them, and re-layouts  1.24 us (5%)
  between operations  0.64 us (3%)
    pallas_call x1, Pallas kernels, local(): pl.pallas_call(functools.partial(program, nx, ny), out_shape=(pltpu.VMEM(...  23.2 us
    unnamed x2, local copies, waits for them, and re-layouts  1.24 us

profile of v3, /device:TPU:0, one launch (start us, length us, event | category | flops | bytes accessed | tf_op | source)
XLA Modules:
  0.0 25.1 jit_solution(5066174768330042099)
XLA Ops:
  0.6 23.2 %chebyshev.1 = (f32[4,2,8,512]{3,2,1,0:T(8,128)S(1)}, f32[4,16]{1,0:T(4,128)S(1)}) custom-call(s32[32]{0:T(128)} %plan_any.1, bf16[2,16,8,512]{3,2,1,0:T(8,128)(2,1)} %stored_any.1, f32[2,8,512]{2,1,0:T(8,128)} %disorder_any.1, s32[2,8,512]{2,1,0:T(8,128)} %vacancy_any.1), custom_call_target="tpu_custom_call" | custom-call | tf_op jit(solution)/shard_map/chebyshev/pallas_call | solution.py:507
  23.8 0.7 %copy.8 = f32[4,2,8,512]{3,2,1,0:T(8,128)} copy(f32[4,2,8,512]{3,2,1,0:T(8,128)S(1)} %get-tuple-element.2) | data formatting | bytes 262144
  24.5 0.6 %copy.9 = f32[4,16]{1,0:T(4,128)} copy(f32[4,16]{1,0:T(4,128)S(1)} %get-tuple-element.3) | data formatting | bytes 512

commit v4 on v3

--- a/solution.py
+++ b/solution.py
@@ -75,6 +75,9 @@
             device_id=device, device_id_type=MESH,
         )
 
+    def drain(span, out_sem, in_sem):
+        return copy(span, span, out_sem, in_sem, at(0, 0))
+
     loads = []
     for t, (source, target) in enumerate((
         (stored_any, stored_ref), (plan_any, plan_ref),
@@ -153,21 +156,20 @@
             edge_send[i] = edge(i)
         edge_recv[gy] = edge(0)
 
-    moves = [[] for _ in range(halves)]
-
     def start_blocks(h):
         for i in range(1, ny):
-            move = copy(send.at[h, i], recv[h].at[gy], a2a_send.at[h, i],
-                        a2a_recv.at[h, i], (gx, peer(i)))
-            move.start()
-            moves[h].append(move)
+            copy(send.at[h, i], recv[h].at[gy], a2a_send.at[h], a2a_recv.at[h],
+                 (gx, peer(i))).start()
 
     def start_edges():
         for i in range(1, ny):
-            move = copy(edge_send.at[i], edge_recv.at[gy], a2a_send.at[halves, i],
-                        a2a_recv.at[halves, i], (gx, peer(i)))
-            move.start()
-            moves[0].append(move)
+            copy(edge_send.at[i], edge_recv.at[gy], a2a_send.at[halves], a2a_recv.at[halves],
+                 (gx, peer(i))).start()
+
+    block_drains = [
+        drain(recv[h].at[0 : ny - 1], a2a_send.at[h], a2a_recv.at[h]) for h in range(halves)
+    ]
+    edge_drain = drain(edge_recv.at[0 : ny - 1], a2a_send.at[halves], a2a_recv.at[halves])
 
     turn(0)
     fill(0)
@@ -198,11 +200,15 @@
         else:
             pl.when(when)(sites[name].start)
 
+    x_drain = drain(site_x, site_send.at[0], site_recv.at[0])
+    y_drain = drain(site_y, site_send.at[1], site_recv.at[1])
+    z_drain = drain(site_z, site_send.at[2], site_recv.at[2])
+
     pl.semaphore_wait(barrier, entered)
     pass_on(0)
     for side, a in enumerate((-1, 1)):
-        site(("x", a), site_send_x.at[side], site_x.at[side], side, at(a, 0), linked[a])
-        site(("y", a), site_edge, site_y.at[side], 2 + side, at(0, a))
+        site(("x", a), site_send_x.at[side], site_x.at[side], 0, at(a, 0), linked[a])
+        site(("y", a), site_edge, site_y.at[side], 1, at(0, a))
     start_blocks(0)
 
     for h in range(1, halves):
@@ -218,8 +224,7 @@
         token_round(step)
     for h in range(1, halves):
         fill(h)
-        for move in moves[h - 1][: ny - 1]:
-            move.wait_send()
+        block_drains[h - 1].wait_send()
         start_blocks(h)
     token_round(nx - 3)
     for a in (-1, 1):
@@ -248,18 +253,17 @@
         onsite[:, rows, 0:long] = energy * scale
 
     site_rows(0, disorder_ref[...], keep_own)
-    for a in (-1, 1):
-        sites["y", a].wait()
+    y_drain.wait()
     site_both[...] = jnp.where((short & (span // 2)) == 0, site_y[0], site_y[1])
     for side, a in enumerate((-1, 1)):
-        site(("z", a), site_both, site_z.at[side], 4 + side, at(a, 0))
+        site(("z", a), site_both, site_z.at[side], 2, at(a, 0))
     site_ends(0, site_both[...])
 
     def far_sites():
+        x_drain.wait()
+        z_drain.wait()
         for side, a in enumerate((-1, 1)):
-            sites["x", a].wait()
             site_rows(a, site_x[side, :, 0:HALO], site_x[side, :, HALO:])
-            sites["z", a].wait()
             site_ends(a, site_z[side])
 
     def begin(h, first, last, edges):
@@ -273,13 +277,18 @@
                 real0[h, s, x, :, 0:long] = rows[own] * mask[:, 0:long]
                 real0[h, s, x, :, long:] = edge[own] * mask[:, long:]
 
-    halos = [{} for _ in range(halves)]
-
-    def halo(h, name, a, source, target, slot):
-        side = 0 if a == -1 else 1
-        halos[h][name, a] = copy(source, target, halo_send.at[h, side, slot],
-                                 halo_recv.at[h, side, slot], at(a, 0))
-        halos[h][name, a].start()
+    near_drains = [
+        drain(lattice.at[h, 0 : 2 * NEAR], halo_send.at[h, 0], halo_recv.at[h, 0])
+        for h in range(halves)
+    ]
+    far_drains = [
+        drain(lattice.at[h, 0 : 2 * NEAR], halo_send.at[h, 1], halo_recv.at[h, 1])
+        for h in range(halves)
+    ]
+    side_drain = drain(edge_side, halo_send.at[0, 2], halo_recv.at[0, 2])
+
+    def halo(h, a, source, target, slot):
+        copy(source, target, halo_send.at[h, slot], halo_recv.at[h, slot], at(a, 0)).start()
 
     def own_edge():
         left = plan_ref[lax.rem(gy * blocks - 1 + ny * blocks, ny * blocks)] // blocks
@@ -293,21 +302,21 @@
             rows_out, rows_in = rows_to(a, wide).start + HALO, rows_from(a, wide).start
             source = lattice.at[h, rows_out + cut.start : rows_out + cut.stop]
             target = lattice.at[h, rows_in + cut.start : rows_in + cut.stop]
-            halo(h, name, a, source, target, 0 if name == "near" else 1)
+            halo(h, a, source, target, 0 if name == "near" else 1)
 
     def arrive(h):
-        for j, move in enumerate(moves[h]):
-            move.wait_recv()
-            if h == halves - 1 or j >= ny - 1:
-                move.wait_send()
+        block_drains[h].wait_recv()
+        if h == halves - 1:
+            block_drains[h].wait_send()
         for k in range(blocks):
             source = plan_ref[gy * blocks + k] // blocks
             lattice[h, HALO : HALO + wide, :, k * BLOCK : (k + 1) * BLOCK] = recv[h][source]
         send_rows(h, "near")
         if h == 0:
+            edge_drain.wait()
             edge_own[...] = own_edge().astype(BF16)
             for a in (1, -1):
-                halo(0, "edge", a, edge_own, edge_side.at[0 if a == -1 else 1], 2)
+                halo(0, a, edge_own, edge_side.at[0 if a == -1 else 1], 2)
         begin(h, HALO, HALO + wide, (own_edge(), 0))
 
     def back(value):
@@ -422,12 +431,11 @@
         return {a: edge_side[0 if a == -1 else 1].astype(F32) for a in (1, -1)}
 
     def near_stage(h):
-        for a in (1, -1):
-            if h == 0:
-                halos[h]["edge", a].wait()
-            halos[h]["near", a].wait_recv()
-            if h < halves - 1:
-                halos[h]["near", a].wait_send()
+        if h == 0:
+            side_drain.wait()
+        near_drains[h].wait_recv()
+        if h < halves - 1:
+            near_drains[h].wait_send()
         edges = halo_edges()
         begin(h, HALO - NEAR, HALO, (edges[1], wide - NEAR))
         begin(h, HALO + wide, HALO + wide + NEAR, (edges[-1], 0))
@@ -436,8 +444,7 @@
         border(2, h)
 
     def far_stage(h):
-        for a in (1, -1):
-            halos[h]["far", a].wait()
+        far_drains[h].wait()
         edges = halo_edges()
         begin(h, 0, HALO - NEAR, (edges[1], wide - HALO))
         begin(h, HALO + wide + NEAR, 2 * HALO + wide, (edges[-1], NEAR))
@@ -468,8 +475,7 @@
         for n in range(1, TERMS):
             inside(n, h)
     far_sites()
-    for a in (1, -1):
-        halos[halves - 1]["near", a].wait_send()
+    near_drains[halves - 1].wait_send()
     for h in range(halves):
         send_rows(h, "far")
     for h in range(halves):
@@ -478,15 +484,11 @@
     part[...] = trace_row
     me = gx * ny + gy
     parts[me] = trace_row
-    sent = []
     for i in range(1, many):
-        move = copy(part, parts.at[me], sum_send.at[i], sum_recv.at[i], at(i // ny, i % ny))
-        move.start()
-        sent.append(move)
+        copy(part, parts.at[me], sum_send.at[0], sum_recv.at[0], at(i // ny, i % ny)).start()
     for h in range(halves):
         far_stage(h)
-    for move in sent:
-        move.wait()
+    drain(parts.at[0 : many - 1], sum_send.at[0], sum_recv.at[0]).wait()
     total = parts[0]
     for p in range(1, many):
         total = total + parts[p]
@@ -497,6 +499,17 @@
         trace_ref[n : n + 1, :] = turned_row[:, :vectors]
 
 
+def store(moments_ref, trace_ref, moments_any, trace_any, sems):
+    copies = [
+        pltpu.make_async_copy(trace_ref, trace_any, sems.at[0]),
+        pltpu.make_async_copy(moments_ref, moments_any, sems.at[1]),
+    ]
+    for move in copies:
+        move.start()
+    for move in copies:
+        move.wait()
+
+
 def local(nx, ny, stored_vectors, disorder, vacancy, plan):
     vectors, wide, long = stored_vectors.shape[1:]
     tall, extent = wide + 2 * HALO, long + BLOCK
@@ -504,7 +517,7 @@
     dma = pltpu.SemaphoreType.DMA
     many = nx * ny
     field = pltpu.VMEM((halves, 2, tall, GROUP, extent), F32)
-    return pl.pallas_call(
+    moments, trace = pl.pallas_call(
         functools.partial(program, nx, ny),
         out_shape=(
             pltpu.VMEM((TERMS, 2, wide, long), F32),
@@ -540,16 +553,29 @@
             pltpu.VMEM((1, BLOCK), F32),
             pltpu.VMEM((many, 1, BLOCK), F32),
             dma((4,)),
-            dma((halves + 1, ny)), dma((halves + 1, ny)),
-            dma((halves, 2, 3)), dma((halves, 2, 3)),
-            dma((6,)), dma((6,)),
-            dma((many,)), dma((many,)),
+            dma((halves + 1,)), dma((halves + 1,)),
+            dma((halves, 3)), dma((halves, 3)),
+            dma((3,)), dma((3,)),
+            dma((1,)), dma((1,)),
             pltpu.SemaphoreType.REGULAR((nx - 2, 2)),
         ]
         + [pltpu.VMEM((ny, wide, pair, BLOCK), BF16)] * halves,
         compiler_params=pltpu.CompilerParams(collective_id=0, has_side_effects=True),
         name="chebyshev",
     )(plan, stored_vectors, disorder, vacancy)
+    moments = pltpu.with_memory_space_constraint(moments, pltpu.VMEM)
+    trace = pltpu.with_memory_space_constraint(trace, pltpu.VMEM)
+    return pl.pallas_call(
+        store,
+        out_shape=(
+            jax.ShapeDtypeStruct(moments.shape, F32),
+            jax.ShapeDtypeStruct(trace.shape, F32),
+        ),
+        in_specs=[pl.BlockSpec(memory_space=pltpu.VMEM)] * 2,
+        out_specs=(pl.BlockSpec(memory_space=pl.ANY),) * 2,
+        scratch_shapes=[dma((2,))],
+        name="store",
+    )(moments, trace)
 
 
 def solution(mesh):

time: 25.2 us -> 23.7 us (0.940)
  local copies, waits for them, and re-layouts: 1.24 us -> 0 us
  Pallas kernels: 23.2 us -> 22.9 us
    unnamed x2 -> x0, local copies, waits for them, and re-layouts: 1.24 us -> none
    pallas_call x1, Pallas kernels: 23.2 us -> 22.2 us  [local(): pl.pallas_call(functools.partial(program, nx, ny), out_shape=(pltpu.VMEM(...]
    pallas_call x0 -> x1, Pallas kernels: none -> 0.68 us  [local(): pl.pallas_call(store, out_shape=(jax.ShapeDtypeStruct(moments.shape, F32)...]
where the time goes in v4:
time: 23.7 us; the launch traced here: 23.5 us
  Pallas kernels  22.9 us (97%)
  between operations  0.64 us (3%)
    pallas_call x1, Pallas kernels, local(): pl.pallas_call(functools.partial(program, nx, ny), out_shape=(pltpu.VMEM(...  22.2 us
    pallas_call x1, Pallas kernels, local(): pl.pallas_call(store, out_shape=(jax.ShapeDtypeStruct(moments.shape, F32)...  0.68 us

profile of v4, /device:TPU:0, one launch (start us, length us, event | category | flops | bytes accessed | tf_op | source)
XLA Modules:
  0.0 23.5 jit_solution(10306437234060048240)
XLA Ops:
  0.6 22.2 %chebyshev.1 = (f32[4,2,8,512]{3,2,1,0:T(8,128)S(1)}, f32[4,16]{1,0:T(4,128)S(1)}) custom-call(s32[32]{0:T(128)} %plan_any.1, bf16[2,16,8,512]{3,2,1,0:T(8,128)(2,1)} %stored_any.1, f32[2,8,512]{2,1,0:T(8,128)} %disorder_any.1, s32[2,8,512]{2,1,0:T(8,128)} %vacancy_any.1), custom_call_target="tpu_custom_call" | custom-call | tf_op jit(solution)/shard_map/chebyshev/pallas_call | solution.py:520
  22.8 0.7 %store.1 = (f32[4,2,8,512]{3,2,1,0:T(8,128)}, f32[4,16]{1,0:T(4,128)}) custom-call(f32[4,2,8,512]{3,2,1,0:T(8,128)S(1)} %get-tuple-element.4.moments_ref, f32[4,16]{1,0:T(4,128)S(1)} %get-tuple-element.5.trace_ref), custom_call_target="tpu_custom_call" | custom-call | tf_op jit(solution)/shard_map/store/pallas_call | solution.py:568

commit v5 on v4

--- a/solution.py
+++ b/solution.py
@@ -40,14 +40,14 @@
     turned, strips, send, edge_send, edge_recv, lattice, edge_own, edge_side,
     site_send_x, site_x, site_edge, site_y, site_both, site_z, keep_ref, onsite, factor,
     real0, real1, real2, real3, imag1, imag2, imag3, sums, traces, part, parts,
-    load_sem, a2a_send, a2a_recv, halo_send, halo_recv, site_send, site_recv, sum_send, sum_recv, token,
+    load_sem, a2a_send, a2a_recv, halo_send, halo_recv, site_send, site_recv, sum_send, sum_recv, direct_send, direct_recv, token,
     *landing,
 ):
     gx, gy = lax.axis_index("gx"), lax.axis_index("gy")
     wide, long = disorder_ref.shape[1], disorder_ref.shape[2]
     halves = lattice.shape[0]
     vectors = halves * GROUP
-    recv = landing
+    recv, near_in = landing[:halves], landing[halves]
     extent = long + BLOCK
     blocks = long // BLOCK
     many = nx * ny
@@ -144,8 +144,10 @@
         right = jnp.where(inside_mine(right), right, 0)
         picks.append((pick, left, right))
 
+    final = halves - 1
+
     def fill(h):
-        for i in range(1, ny):
+        for i in range(0 if h == final else 1, ny):
             send[h, i] = turned[h, picks[i][0]]
         recv[h][gy] = turned[h, picks[0][0]]
 
@@ -160,6 +162,12 @@
         for i in range(1, ny):
             copy(send.at[h, i], recv[h].at[gy], a2a_send.at[h], a2a_recv.at[h],
                  (gx, peer(i))).start()
+
+    def start_direct(a):
+        rows = slice(wide - NEAR, wide) if a == 1 else slice(0, NEAR)
+        for i in range(ny):
+            copy(send.at[final, i, rows], near_in.at[gy], direct_send.at[0], direct_recv.at[0],
+                 (lax.rem(gx + a + nx, nx), peer(i))).start()
 
     def start_edges():
         for i in range(1, ny):
@@ -204,20 +212,20 @@
     y_drain = drain(site_y, site_send.at[1], site_recv.at[1])
     z_drain = drain(site_z, site_send.at[2], site_recv.at[2])
 
+    for h in range(1, halves):
+        turn(h)
+    fill_edges()
     pl.semaphore_wait(barrier, entered)
+    start_edges()
     pass_on(0)
     for side, a in enumerate((-1, 1)):
         site(("x", a), site_send_x.at[side], site_x.at[side], 0, at(a, 0), linked[a])
         site(("y", a), site_edge, site_y.at[side], 1, at(0, a))
     start_blocks(0)
 
-    for h in range(1, halves):
-        turn(h)
-    fill_edges()
-    start_edges()
     def token_round(step):
         hear(step)
-        if step < nx - 3:
+        if step < nx - 2:
             pass_on(step + 1)
 
     for step in range(nx - 3):
@@ -225,10 +233,11 @@
     for h in range(1, halves):
         fill(h)
         block_drains[h - 1].wait_send()
+        if h == final:
+            token_round(nx - 3)
+            for a in (-1, 1):
+                pl.when(~linked[a])(sites["x", a].start)
         start_blocks(h)
-    token_round(nx - 3)
-    for a in (-1, 1):
-        pl.when(~linked[a])(sites["x", a].start)
 
     short = lax.broadcasted_iota(jnp.int32, (2, 1, BLOCK), 2)
 
@@ -285,10 +294,17 @@
         drain(lattice.at[h, 0 : 2 * NEAR], halo_send.at[h, 1], halo_recv.at[h, 1])
         for h in range(halves)
     ]
+    inner = linked[-1] & linked[1]
+    one_drain = drain(lattice.at[final, 0:NEAR], halo_send.at[final, 0], halo_recv.at[final, 0])
+    direct_drain = drain(near_in, direct_send.at[0], direct_recv.at[0])
     side_drain = drain(edge_side, halo_send.at[0, 2], halo_recv.at[0, 2])
 
-    def halo(h, a, source, target, slot):
-        copy(source, target, halo_send.at[h, slot], halo_recv.at[h, slot], at(a, 0)).start()
+    def halo(h, a, source, target, slot, when=None):
+        move = copy(source, target, halo_send.at[h, slot], halo_recv.at[h, slot], at(a, 0))
+        if when is None:
+            move.start()
+        else:
+            pl.when(when)(move.start)
 
     def own_edge():
         left = plan_ref[lax.rem(gy * blocks - 1 + ny * blocks, ny * blocks)] // blocks
@@ -302,7 +318,8 @@
             rows_out, rows_in = rows_to(a, wide).start + HALO, rows_from(a, wide).start
             source = lattice.at[h, rows_out + cut.start : rows_out + cut.stop]
             target = lattice.at[h, rows_in + cut.start : rows_in + cut.stop]
-            halo(h, a, source, target, 0 if name == "near" else 1)
+            relayed = linked[a] if h == final and name == "near" else None
+            halo(h, a, source, target, 0 if name == "near" else 1, relayed)
 
     def arrive(h):
         block_drains[h].wait_recv()
@@ -317,6 +334,10 @@
             edge_own[...] = own_edge().astype(BF16)
             for a in (1, -1):
                 halo(0, a, edge_own, edge_side.at[0 if a == -1 else 1], 2)
+        if h == 0:
+            token_round(nx - 2)
+            for a in (-1, 1):
+                pl.when(~linked[a])(functools.partial(start_direct, a))
         begin(h, HALO, HALO + wide, (own_edge(), 0))
 
     def back(value):
@@ -433,9 +454,20 @@
     def near_stage(h):
         if h == 0:
             side_drain.wait()
-        near_drains[h].wait_recv()
-        if h < halves - 1:
-            near_drains[h].wait_send()
+        if h < final:
+            near_drains[h].wait()
+        else:
+            pl.when(inner)(near_drains[h].wait_recv)
+            pl.when(~inner)(one_drain.wait_recv)
+            pl.when(~inner)(direct_drain.wait)
+
+            def land(start):
+                for k in range(blocks):
+                    source = plan_ref[gy * blocks + k] // blocks
+                    lattice[h, start : start + NEAR, :, k * BLOCK : (k + 1) * BLOCK] = near_in[source]
+
+            pl.when(~linked[-1])(functools.partial(land, HALO - NEAR))
+            pl.when(~linked[1])(functools.partial(land, HALO + wide))
         edges = halo_edges()
         begin(h, HALO - NEAR, HALO, (edges[1], wide - NEAR))
         begin(h, HALO + wide, HALO + wide + NEAR, (edges[-1], 0))
@@ -472,12 +504,14 @@
     trace_row = jnp.zeros((1, BLOCK), F32)
     for h in range(halves):
         arrive(h)
+        if h == final:
+            for later in range(halves):
+                send_rows(later, "far")
         for n in range(1, TERMS):
             inside(n, h)
     far_sites()
-    near_drains[halves - 1].wait_send()
-    for h in range(halves):
-        send_rows(h, "far")
+    pl.when(inner)(near_drains[final].wait_send)
+    pl.when(~inner)(one_drain.wait_send)
     for h in range(halves):
         near_stage(h)
         trace_row = trace_row + gather_traces(h)
@@ -557,9 +591,12 @@
             dma((halves, 3)), dma((halves, 3)),
             dma((3,)), dma((3,)),
             dma((1,)), dma((1,)),
-            pltpu.SemaphoreType.REGULAR((nx - 2, 2)),
+            dma((1,)), dma((1,)),
+            pltpu.SemaphoreType.REGULAR((nx - 1, 2)),
+
         ]
-        + [pltpu.VMEM((ny, wide, pair, BLOCK), BF16)] * halves,
+        + [pltpu.VMEM((ny, wide, pair, BLOCK), BF16)] * halves
+        + [pltpu.VMEM((ny, NEAR, pair, BLOCK), BF16)],
         compiler_params=pltpu.CompilerParams(collective_id=0, has_side_effects=True),
         name="chebyshev",
     )(plan, stored_vectors, disorder, vacancy)

time: 23.7 us -> 23.2 us (0.979)
  Pallas kernels: 22.9 us -> 22.5 us
    pallas_call x1, Pallas kernels: 22.2 us -> 21.8 us  [local(): pl.pallas_call(functools.partial(program, nx, ny), out_shape=(pltpu.VMEM(...]
where the time goes in v5:
time: 23.2 us; the launch traced here: 23.1 us
  Pallas kernels  22.5 us (97%)
  between operations  0.64 us (3%)
    pallas_call x1, Pallas kernels, local(): pl.pallas_call(functools.partial(program, nx, ny), out_shape=(pltpu.VMEM(...  21.8 us
    pallas_call x1, Pallas kernels, local(): pl.pallas_call(store, out_shape=(jax.ShapeDtypeStruct(moments.shape, F32)...  0.68 us

profile of v5, /device:TPU:0, one launch (start us, length us, event | category | flops | bytes accessed | tf_op | source)
XLA Modules:
  0.0 23.1 jit_solution(12665064544005269138)
XLA Ops:
  0.6 21.8 %chebyshev.1 = (f32[4,2,8,512]{3,2,1,0:T(8,128)S(1)}, f32[4,16]{1,0:T(4,128)S(1)}) custom-call(s32[32]{0:T(128)} %plan_any.1, bf16[2,16,8,512]{3,2,1,0:T(8,128)(2,1)} %stored_any.1, f32[2,8,512]{2,1,0:T(8,128)} %disorder_any.1, s32[2,8,512]{2,1,0:T(8,128)} %vacancy_any.1), custom_call_target="tpu_custom_call" | custom-call | tf_op jit(solution)/shard_map/chebyshev/pallas_call | solution.py:554
  22.4 0.7 %store.1 = (f32[4,2,8,512]{3,2,1,0:T(8,128)}, f32[4,16]{1,0:T(4,128)}) custom-call(f32[4,2,8,512]{3,2,1,0:T(8,128)S(1)} %get-tuple-element.4.moments_ref, f32[4,16]{1,0:T(4,128)S(1)} %get-tuple-element.5.trace_ref), custom_call_target="tpu_custom_call" | custom-call | tf_op jit(solution)/shard_map/store/pallas_call | solution.py:605
